TPU v7x, 16 devices: a 4x2x1 block of a 4x4x8 slice. The times are simulated.
16 devices in a mesh: req: 2 (over y, z), cp: 8 (over x, core).
Axes of the slice: x: 4, y: 2, z: 1, core: 2. Of those that a mesh axis runs over, the one named last changes fastest.
The devices are a block of a 4x4x8 slice.
Arguments:
- hidden: bfloat16 [8192, 2048], P(('req', 'cp')), parts along dimension 0
- positions: int32 [8192], P(('req', 'cp')), parts along dimension 0
- gain_attn: bfloat16 [2, 2048], replicated
- gain_mlp: bfloat16 [2, 2048], replicated
- w_query: bfloat16 [2, 2048, 16, 128], replicated
- w_key: bfloat16 [2, 2048, 16, 128], replicated
- w_value: bfloat16 [2, 2048, 16, 128], replicated
- w_out: bfloat16 [2, 16, 128, 2048], replicated
- w_gate: bfloat16 [2, 2048, 8192], replicated
- w_up: bfloat16 [2, 2048, 8192], replicated
- w_down: bfloat16 [2, 8192, 2048], replicated
Outputs:
- output 1: bfloat16 [8192, 2048], P(('req', 'cp')), parts along dimension 0
- output 2: bfloat16 [2, 8192, 16, 128], P(None, 'req', 'cp'), parts along dimension 1
- output 3: bfloat16 [2, 8192, 16, 128], P(None, 'req', 'cp'), parts along dimension 1
There are 2 independent parts. A program takes and returns all parts, laid end to end along the dimension named above; an argument that names none is the same for every part.
All inputs are finite; a program needn't handle non-finite values.
Results may differ from a plain program's by a relative error of at most 0.016795.
Values are sent between devices in bfloat16 or wider.
A program may use at most 768 MiB of HBM per device.

v0:
```python
import functools

import jax
import jax.numpy as jnp
from jax import lax
from jax.experimental import pallas as pl
from jax.experimental.pallas import tpu as pltpu
from jax.sharding import PartitionSpec as P

NORM_EPS = 1e-5
ROPE_BASE = 10000.0
LOG2E = 1.4426950408889634
MESH = pl.DeviceIdType.MESH
MIB = 1024 * 1024
TQ = 512
TK = 1024
SLOTS = 7
TF = 512
BF16, F32 = jnp.bfloat16, jnp.float32


def rms_norm(values, gain_vec):
    wide_vals = values.astype(F32)
    inv_rms = lax.rsqrt(jnp.mean(wide_vals * wide_vals, axis=-1, keepdims=True) + NORM_EPS)
    return (wide_vals * inv_rms * gain_vec.astype(F32)).astype(BF16)


def greet_all(n, me):
    barrier = pltpu.get_barrier_semaphore()
    for d in range(1, n):
        pl.semaphore_signal(barrier, inc=1, device_id={"cp": lax.rem(me + d, n)}, device_id_type=MESH)
    pl.semaphore_wait(barrier, n - 1)


def front_kernel(
    n, heads, dim, layer, first, more, x_ref, gain_ref, *refs
):
    if first:
        pos_ref, freq_ref, *refs = refs
    else:
        cos_in, sin_in, w_in, ha_ref, *refs = refs
    wq_ref, wk_ref, wv_ref, o_ref, k_out, v_out, *refs = refs
    if first:
        cos_out, sin_out, *refs = refs
    if more:
        w_out, w_next, *refs = refs
    if first:
        pos_buf, pos_send, pos_recv, *refs = refs
    else:
        ha_sem, *refs = refs
    h_buf, w_raw, w_buf, q_ref, k_ref, v_ref, vt_ref, cos_ref, sin_ref, o_buf, m_st, l_st, acc_st, *sems = refs
    in_sem, out_sem, w_sem, recv_sem, own_sem, fwd_sem, relay_sem, o_local, o_send, o_recv = sems
    block, model = h_buf.shape[2:]
    rows = n * block
    piece = block // 2
    width = heads * dim
    scale = LOG2E * dim**-0.5
    chips = n // 2
    me = lax.axis_index("cp")
    chip, core = me // 2, lax.rem(me, 2)

    def at(step, k):
        return 2 * lax.rem(chip + step, chips) + k

    right, left, opp, partner = at(1, core), at(chips - 1, core), at(2, core), at(0, 1 - core)
    sources = (left, right, opp)

    def remote(s, origin, p, target, sem):
        part = h_buf.at[s, origin, pl.ds(p * piece, piece)]
        return pltpu.make_async_remote_copy(
            src_ref=part, dst_ref=part, send_sem=sem, recv_sem=recv_sem.at[s, origin, p],
            device_id={"cp": target}, device_id_type=MESH,
        )

    own_sends = [(right, 0), (left, 1), (right, 1), (left, 0), (partner, 0), (partner, 1)]

    def send_own(s):
        for j, (target, p) in enumerate(own_sends):
            remote(s, me, p, target, own_sem.at[s, j]).start()

    def arrived(s, origin, p):
        remote(s, origin, p, partner, own_sem.at[s, 0]).wait_recv()

    def relay(s, j, p):
        return remote(s, sources[j], p, partner, relay_sem.at[s, j, p])

    def forward(s, way):
        return remote(s, (left, right)[way], way, (right, left)[way], fwd_sem.at[s, way])

    def pass_on(s):
        for way in range(2):
            arrived(s, (left, right)[way], way)
            forward(s, way).start()
            relay(s, way, way).start()

    def receive(s, k):
        @pl.when(k == 0)
        def _():
            for p in range(2):
                arrived(s, partner, p)

        @pl.when(k == 1)
        def _():
            for way in range(2):
                arrived(s, (left, right)[way], 1 - way)
                relay(s, way, 1 - way).start()
            for p in range(2):
                arrived(s, at(chips - 1, 1 - core), p)

        @pl.when(k == 2)
        def _():
            for p in range(2):
                arrived(s, at(1, 1 - core), p)

        @pl.when(k == 3)
        def _():
            for p in range(2):
                arrived(s, opp, p)
                relay(s, 2, p).start()
            for p in range(2):
                arrived(s, at(2, 1 - core), p)

    def ready(k):
        c = lax.rem(chip + (0, chips - 1, 1, 2)[k], chips)
        return pltpu.make_async_copy(ha_ref.at[pl.ds(2 * c, 2)], h_buf.at[0, pl.ds(2 * c, 2)], ha_sem.at[k])

    def place(s, d):
        return pl.multiple_of(jnp.where(s == 0, d * block, rows + (n - 1 - d) * block), block)

    def project(s, c):
        h = h_buf[s, pl.ds(2 * c, 2)].reshape(2 * block, model)
        key, val, query = (
            jnp.dot(h, w_buf[:, j * width : (j + 1) * width], preferred_element_type=F32) for j in (1, 2, 0)
        )
        for j in range(2):
            part = pl.ds(place(s, 2 * c + j), block)
            cos, sin = cos_ref[part, :], sin_ref[part, :]
            mine = slice(j * block, (j + 1) * block)
            for g in range(heads):
                lo, hi = g * dim, (g + 1) * dim
                for y, dst in ((key, k_ref), (query, q_ref)):
                    x = y[mine, lo:hi]
                    dst[part, lo:hi] = (x * cos + pltpu.roll(x, dim // 2, 1) * sin).astype(BF16)
            v_ref[part, :] = val[mine].astype(BF16)
            vt_ref[:, part] = val[mine].T.astype(BF16)

    def scores_of(queries, g, start, size, masked):
        k = k_ref[pl.ds(start, size), g * dim : (g + 1) * dim]
        s = lax.dot_general(k, queries[g], (((1,), (1,)), ((), ())), preferred_element_type=F32)
        if masked:
            row = lax.broadcasted_iota(jnp.int32, s.shape, 0)
            col = lax.broadcasted_iota(jnp.int32, s.shape, 1)
            s = jnp.where(row <= col, s, -jnp.inf)
        return s

    def absorb(g, s, start, size, state):
        m, l, acc = state
        m_new = jnp.maximum(m, jnp.max(s, axis=0, keepdims=True))
        a = jnp.exp2((m - m_new) * scale)
        p = jnp.exp2((s - m_new) * scale)
        l = l * a + jnp.sum(p, axis=0, keepdims=True)
        vt = vt_ref[g * dim : (g + 1) * dim, pl.ds(start, size)]
        return m_new, l, acc * a + jnp.dot(vt, p.astype(BF16), preferred_element_type=F32)

    def run(queries, parts, carry):
        carry = list(carry)
        items = [(g,) + part for part in parts for g in range(heads)]
        scores = [scores_of(queries, *item) for item in items[:2]]
        for j, (g, start, size, _) in enumerate(items):
            if j + 2 < len(items):
                scores.append(scores_of(queries, *items[j + 2]))
            carry[g] = absorb(g, scores[j], start, size, carry[g])
        return tuple(carry)

    def chunk(queries, start, size, carry, masked):
        return run(queries, [(start, size, masked)], carry)

    def chunks(queries, lo, hi, base, size, carry):
        return lax.fori_loop(
            lo, hi, lambda j, c: chunk(queries, pl.multiple_of(base + j * size, size), size, c, False), carry
        )

    def queries_at(start):
        return [q_ref[pl.ds(start, TQ), g * dim : (g + 1) * dim] for g in range(heads)]

    def fresh():
        return tuple(
            (jnp.full((1, TQ), -jnp.inf, F32), jnp.zeros((1, TQ), F32), jnp.zeros((dim, TQ), F32)) for _ in range(heads)
        )

    def finish(t, base, carry):
        start = pl.multiple_of(base + t * TQ, TQ)
        queries = queries_at(start)
        per = TK // TQ
        full = t // per
        carry = chunks(queries, 0, full, base, TK, carry)
        carry = chunks(queries, full * per, t, base, TQ, carry)
        carry = chunk(queries, start, TQ, carry, True)
        for g in range(heads):
            m, l, acc = carry[g]
            o_buf[pl.ds(start, TQ), g * dim : (g + 1) * dim] = (acc / l).T.astype(BF16)

    outs = (o_ref.at[0], o_ref.at[1])
    gathers = (0, 1) if first else (1,)

    def own_result(s):
        cols = pl.ds(pl.multiple_of(me * width, width), width)
        return pltpu.make_async_copy(o_buf.at[pl.ds(place(s, me), block), :], outs[s].at[:, cols], o_local.at[s])

    def result(s, d, source):
        cols = pl.ds(pl.multiple_of(source * width, width), width)
        return pltpu.make_async_remote_copy(
            src_ref=o_buf.at[pl.ds(place(s, d), block), :], dst_ref=outs[s].at[:, cols],
            send_sem=o_send.at[s, d], recv_sem=o_recv.at[s, source],
            device_id={"cp": d}, device_id_type=MESH,
        )

    def weights(of, j):
        return pltpu.make_async_copy((wq_ref, wk_ref, wv_ref)[j].at[of, :, me], w_raw.at[j], w_sem.at[j])

    def unpack(dst):
        per = model // 256

        def step(i, _):
            j, part = i // per, pl.ds(pl.multiple_of(lax.rem(i, per) * 256, 256), 256)
            w = w_raw[j, part]
            for g in range(heads):
                dst[part, pl.ds(pl.multiple_of(j * width + g * dim, dim), dim)] = w[:, g, :]
            return 0

        lax.fori_loop(0, 3 * per, step, 0)

    if first:
        loads = [weights(layer, j) for j in range(3)]
    else:
        loads = [
            pltpu.make_async_copy(src, dst, in_sem.at[j])
            for j, (src, dst) in enumerate(((cos_in, cos_ref), (sin_in, sin_ref), (w_in, w_buf)))
        ] + ([weights(layer + 1, j) for j in range(3)] if more else [])
    for load in loads:
        load.start()
    if not first:
        for k in range(chips):
            ready(k).start()
    for s in gathers:
        h_buf[s, me] = rms_norm(x_ref[s * block : (s + 1) * block, :], gain_ref[layer : layer + 1, :])
    greet_all(n, me)
    if first:
        def pos_copy(d, slot):
            return pltpu.make_async_remote_copy(
                src_ref=pos_ref, dst_ref=pos_buf.at[slot], send_sem=pos_send.at[d], recv_sem=pos_recv.at[slot],
                device_id={"cp": lax.rem(me + d, n)}, device_id_type=MESH,
            )

        for d in range(1, n):
            pos_copy(d, me).start()
    send_own(gathers[0])
    if first:
        pos_buf[me] = pos_ref[...]
    for j in range(3):
        loads[j].wait()
    if first:
        unpack(w_buf)
        if more:
            for j in range(3):
                weights(layer + 1, j).start()
        pass_on(0)
        send_own(1)
    if more:
        for j in range(3):
            weights(layer + 1, j).wait()
        unpack(w_next)
        for d in range(1, n):
            pos_copy(d, me).wait_send()
            pos_copy(d, lax.rem(me + d, n)).wait_recv()
        sign = jnp.where(lax.broadcasted_iota(jnp.int32, (1, dim), 1) < dim // 2, -1.0, 1.0).astype(F32)

        def tables(s, c):
            per = block // 128

            def step(i, _):
                d, j = 2 * c + i // per, lax.rem(i, per)
                pos = pos_buf[d, pl.ds(s * per + j, 1), :].astype(F32)
                angles = jnp.broadcast_to(pos, (128, 128)).T * freq_ref[...]
                part = pl.ds(pl.multiple_of(place(s, d) + j * 128, 128), 128)
                cos_ref[part, :] = jnp.cos(angles)
                sin_ref[part, :] = jnp.sin(angles) * sign
                return 0

            lax.fori_loop(0, 2 * per, step, 0)

    saves = [(k_ref, k_out), (v_ref, v_out)]
    if first:
        saves += [(cos_ref, cos_out), (sin_ref, sin_out)]
    if more:
        saves.append((w_next, w_out))

    def save(j):
        return pltpu.make_async_copy(*saves[j], out_sem.at[j])

    def half(s, _):
        @pl.when(s == 1)
        def _():
            if first:
                pass_on(1)
            own_result(0).start()
            for d in range(1, n):
                result(0, lax.rem(me + d, n), me).start()

        def step(k, _):
            c = lax.rem(chip + jnp.where(k == 0, 0, jnp.where(k == 1, chips - 1, k - 1)), chips)
            if first:
                tables(s, c)
                receive(s, k)
            else:
                for j in range(chips):

                    @pl.when((s == 0) & (k == j))
                    def _(j=j):
                        ready(j).wait()

                @pl.when(s == 1)
                def _():
                    receive(1, k)

            project(s, c)

            def put(t, carry):
                for g in range(heads):
                    m_st[t, g], l_st[t, g], acc_st[t, g] = carry[g]

            @pl.when(s == 0)
            def _():
                put(c, fresh())

            @pl.when(s == 1)
            def _():
                t = chips - 1 - c
                queries = queries_at(pl.multiple_of(rows + t * TQ, TQ))
                put(t, run(queries, [(j * TK, TK, False) for j in range(rows // TK)], fresh()))

            return 0

        lax.fori_loop(0, chips, step, 0)
        if not first:

            @pl.when(s == 0)
            def _():
                pass_on(1)

        @pl.when(s == 1)
        def _():
            for j in range(len(saves)):
                save(j).start()

        def tile(i, _):
            t = lax.rem(i + chip, chips)
            finish(t, s * rows, tuple((m_st[t, g], l_st[t, g], acc_st[t, g]) for g in range(heads)))

            @pl.when(s == 1)
            def _():
                for j in range(2):
                    d = n - 1 - (2 * t + j)

                    @pl.when(d == me)
                    def _():
                        own_result(1).start()

                    @pl.when(d != me)
                    def _():
                        result(1, d, me).start()

            return 0

        lax.fori_loop(0, chips, tile, 0)
        return 0

    lax.fori_loop(0, 2, half, 0)
    for j in range(len(saves)):
        save(j).wait()
    for s in gathers:
        for j, (target, p) in enumerate(own_sends):
            remote(s, me, p, target, own_sem.at[s, j]).wait_send()
        for way in range(2):
            forward(s, way).wait_send()
        for j in range(3):
            for p in range(2):
                relay(s, j, p).wait_send()
    for s in range(2):
        own_result(s).wait()
        for d in range(1, n):
            other = lax.rem(me + d, n)
            result(s, other, me).wait_send()
            result(s, other, other).wait_recv()


def front(x, gain, tables, w_query, w_key, w_value, n, layer):
    first = layer == 0
    rows, model = x.shape
    num_layers, _, all_heads, dim = w_query.shape
    more = layer < num_layers - 1
    heads = all_heads // n
    width = heads * dim
    block = rows // 2
    seq = n * rows
    vmem = pl.BlockSpec(memory_space=pltpu.VMEM)
    hbm = pl.BlockSpec(memory_space=pl.ANY)
    chips = n // 2
    out = jax.ShapeDtypeStruct((2, block, all_heads * dim), BF16)
    kv = jax.ShapeDtypeStruct((seq, width), BF16)
    table = jax.ShapeDtypeStruct((seq, dim), F32)
    packed = jax.ShapeDtypeStruct((model, 3 * width), BF16)
    dma = pltpu.SemaphoreType.DMA
    pos_scratch = [pltpu.VMEM((n,) + tables[0].shape, jnp.int32), dma((n,)), dma((n,))] if first else [dma((chips,))]
    by_head = [w.reshape(num_layers, model, n, heads, dim) for w in (w_query, w_key, w_value)]
    return pl.pallas_call(
        functools.partial(front_kernel, n, heads, dim, layer, first, more),
        name="front",
        out_shape=[out, kv, kv] + [table, table] * first + [packed] * more,
        in_specs=[vmem] * (4 if first else 2) + [hbm] * (3 if first else 7),
        out_specs=[hbm] * (3 + 2 * first + more),
        scratch_shapes=[pltpu.VMEM(packed.shape, BF16)] * more
        + pos_scratch
        + [
            pltpu.VMEM((2, n, block, model), BF16),
            pltpu.VMEM((3, model, heads, dim), BF16),
            pltpu.VMEM((model, 3 * width), BF16),
            pltpu.VMEM((seq, width), BF16),
            pltpu.VMEM((seq, width), BF16),
            pltpu.VMEM((seq, width), BF16),
            pltpu.VMEM((width, seq), BF16),
            pltpu.VMEM((seq, dim), F32),
            pltpu.VMEM((seq, dim), F32),
            pltpu.VMEM((seq, width), BF16),
            pltpu.VMEM((chips, heads, 1, TQ), F32),
            pltpu.VMEM((chips, heads, 1, TQ), F32),
            pltpu.VMEM((chips, heads, dim, TQ), F32),
            dma((3,)),
            dma((5,)),
            dma((3,)),
            dma((2, n, 2)),
            dma((2, 6)),
            dma((2, 2)),
            dma((2, 3, 2)),
            dma((2,)),
            dma((2, n)),
            dma((2, n)),
        ],
        compiler_params=pltpu.CompilerParams(vmem_limit_bytes=62 * MIB, collective_id=layer + 1, has_side_effects=True),
        cost_estimate=pl.CostEstimate(flops=6 * seq * model * width + 2 * seq * seq * width, bytes_accessed=seq * model * 2, transcendentals=seq * seq * heads // 2),
    )(x, gain, *tables, *by_head)


def mlp_parts(acc, normed, act, wg_ref, wu_ref, wd_ref, now):
    def gate_up(slot=0):
        h = normed[...]
        gate = jnp.dot(h, wg_ref[slot], preferred_element_type=F32)
        up = jnp.dot(h, wu_ref[slot], preferred_element_type=F32)
        act[now] = (jax.nn.silu(gate) * up).astype(BF16)

    def down(slot=0):
        acc[...] += jnp.dot(act[1 - now], wd_ref[slot], preferred_element_type=F32)

    return gate_up, down


def out_step(r, out_steps, layer, x_ref, o_ref, wo_ref, gain_ref, acc, normed):
    o = o_ref[...].reshape(acc.shape[0], o_ref.shape[2])
    part = jnp.dot(o, wo_ref[0], preferred_element_type=F32)

    @pl.when(r == 0)
    def _():
        acc[...] = part

    @pl.when(r > 0)
    def _():
        acc[...] += part

    @pl.when(r == out_steps - 1)
    def _():
        x = (x_ref[...].astype(F32) + acc[...]).astype(BF16)
        normed[...] = rms_norm(x, gain_ref[layer : layer + 1, :])
        acc[...] = x.astype(F32)


def last_kernel(
    out_steps, layer, x_ref, o_ref, wo_ref, gain_ref, wg_ref, wu_ref, wd_ref, *refs
):
    kv_refs = refs[: 2 * (layer + 1)]
    y_ref, kc_ref, vc_ref, acc, normed, act, mixed = refs[2 * (layer + 1) :]
    i = pl.program_id(0)
    last = pl.num_programs(0) - 1
    gate_up, down = mlp_parts(acc, normed, act, wg_ref, wu_ref, wd_ref, lax.rem(i, 2))

    @pl.when(i < out_steps)
    def _():
        out_step(i, out_steps, layer, x_ref, o_ref, wo_ref, gain_ref, acc, normed)

    def caches():
        dim = kc_ref.shape[2]
        for j, src in enumerate(kv_refs):
            count, heads = src.shape[0], src.shape[1] // dim
            for g in range(heads):
                mixed[j, pl.ds(g, count, stride=heads), :] = src[:, g * dim : (g + 1) * dim].astype(F32)
            (kc_ref, vc_ref)[j % 2][j // 2] = mixed[j].astype(BF16)

    @pl.when(i == out_steps)
    def _():
        gate_up()
        caches()

    @pl.when((i > out_steps) & (i < last))
    def _():
        down()
        gate_up()
        caches()

    @pl.when(i == last)
    def _():
        down()
        y_ref[...] = acc[...].astype(BF16)


def split_kernel(
    n, out_steps, layer, steps, x_ref, o_ref, wo_ref, gain_ref, next_gain_ref, wg_ref, wu_ref, wd_ref,
    y_ref, ha_ref, acc, normed, act, mine, wg_buf, wu_buf, wd_buf, w_sem, local_sem, recv_sem, own_sem, fwd_sem, relay_sem,
):
    i = pl.program_id(0)
    s, r = i // steps, lax.rem(i, steps)
    gate_up, down = mlp_parts(acc, normed, act, wg_buf, wu_buf, wd_buf, lax.rem(i, 2))
    slots, tf = wd_buf.shape[:2]
    slices = steps - out_steps - 1

    def load(kind, f):
        cols = pl.ds(pl.multiple_of(f * tf, tf), tf)
        src = (wg_ref.at[layer, :, cols], wu_ref.at[layer, :, cols], wd_ref.at[layer, cols])[kind]
        slot = lax.rem(f, slots)
        return pltpu.make_async_copy(src, (wg_buf, wu_buf, wd_buf)[kind].at[slot], w_sem.at[kind, slot])

    def slice_at(j):
        return jnp.where(s == 0, j, slices - 1 - j)

    def await_loads(kinds, f):
        @pl.when((s == 0) | (f < slices - slots))
        def _():
            for kind in kinds:
                load(kind, f).wait()

    def refill(kinds, f):
        after = jnp.where(s == 0, f + slots, f - slots)

        @pl.when((after >= 0) & (after < slices))
        def _():
            for kind in kinds:
                load(kind, after).start()

    f_up = slice_at(r - out_steps)
    f_down = slice_at(r - out_steps - 1)

    @pl.when(i == 0)
    def _():
        for f in range(slots):
            for kind in range(3):
                load(kind, f).start()
    piece = mine.shape[0] // 2
    chips = n // 2
    me = lax.axis_index("cp")
    chip, core = me // 2, lax.rem(me, 2)

    def at(step, k):
        return 2 * lax.rem(chip + step, chips) + k

    right, left, opp, partner = at(1, core), at(chips - 1, core), at(2, core), at(0, 1 - core)
    sources = (left, right, opp)
    own_sends = [(right, 0), (left, 1), (right, 1), (left, 0), (partner, 0), (partner, 1)]
    barrier = pltpu.get_barrier_semaphore()

    def remote(src, origin, p, target, sem):
        return pltpu.make_async_remote_copy(
            src_ref=src, dst_ref=ha_ref.at[origin, pl.ds(p * piece, piece)], send_sem=sem,
            recv_sem=recv_sem.at[origin, p], device_id={"cp": target}, device_id_type=MESH,
        )

    def held(origin, p):
        return ha_ref.at[origin, pl.ds(p * piece, piece)]

    def own(j):
        target, p = own_sends[j]
        return remote(mine.at[pl.ds(p * piece, piece)], me, p, target, own_sem.at[j])

    def keep():
        return pltpu.make_async_copy(mine, ha_ref.at[me], local_sem)

    def arrived(origin, p):
        remote(held(origin, p), origin, p, partner, own_sem.at[0]).wait_recv()

    def relay(j, p):
        return remote(held(sources[j], p), sources[j], p, partner, relay_sem.at[j, p])

    def forward(way):
        origin = (left, right)[way]
        return remote(held(origin, way), origin, way, (right, left)[way], fwd_sem.at[way])

    @pl.when(i == 0)
    def _():
        for d in range(1, n):
            pl.semaphore_signal(barrier, inc=1, device_id={"cp": lax.rem(me + d, n)}, device_id_type=MESH)
        pl.semaphore_wait(barrier, n - 1)

    @pl.when(i == steps + out_steps + 5)
    def _():
        for way in range(2):
            arrived((left, right)[way], way)
            forward(way).start()
            relay(way, way).start()

    @pl.when(i == steps + out_steps + 11)
    def _():
        for way in range(2):
            arrived((left, right)[way], 1 - way)
            relay(way, 1 - way).start()

    @pl.when(i == 2 * steps - 1)
    def _():
        for p in range(2):
            arrived(opp, p)
            relay(2, p).start()

    @pl.when(r < out_steps)
    def _():
        out_step(r, out_steps, layer, x_ref, o_ref, wo_ref, gain_ref, acc, normed)

    @pl.when((r >= out_steps) & (r < steps - 1))
    def _():
        await_loads((0, 1), f_up)

    @pl.when(r > out_steps)
    def _():
        await_loads((2,), f_down)

    @pl.when(r == out_steps)
    def _():
        gate_up(lax.rem(f_up, slots))

    @pl.when((r > out_steps) & (r < steps - 1))
    def _():
        down(lax.rem(f_down, slots))
        gate_up(lax.rem(f_up, slots))

    @pl.when(r == steps - 1)
    def _():
        down(lax.rem(f_down, slots))
        y_ref[...] = acc[...].astype(BF16)

    @pl.when((r >= out_steps) & (r < steps - 1))
    def _():
        refill((0, 1), f_up)

    @pl.when(r > out_steps)
    def _():
        refill((2,), f_down)

    @pl.when(i == steps - 1)
    def _():
        mine[...] = rms_norm(y_ref[...], next_gain_ref[layer + 1 : layer + 2, :])
        keep().start()
        for j in range(len(own_sends)):
            own(j).start()

    @pl.when(i == 2 * steps - 1)
    def _():
        keep().wait()
        for j in range(len(own_sends)):
            own(j).wait_send()
        for way in range(2):
            forward(way).wait_send()
        for j in range(3):
            for p in range(2):
                relay(j, p).wait_send()
        for origin in (partner, at(chips - 1, 1 - core), at(1, 1 - core), at(2, 1 - core)):
            for p in range(2):
                arrived(origin, p)


def tail_specs(layer, out_steps, slices, tf, model, step, r_of):
    out_at = lambda i: jnp.minimum(r_of(i), out_steps - 1)
    mlp_at = lambda i: jnp.clip(r_of(i) - out_steps, 0, slices - 1)
    down_at = lambda i: jnp.clip(r_of(i) - out_steps - 1, 0, slices - 1)
    w_out = pl.BlockSpec((1, step, model), lambda i: (layer, out_at(i), 0))
    mlp = [
        pl.BlockSpec((1, model, tf), lambda i: (layer, 0, mlp_at(i))),
        pl.BlockSpec((1, model, tf), lambda i: (layer, 0, mlp_at(i))),
        pl.BlockSpec((1, tf, model), lambda i: (layer, down_at(i), 0)),
    ]
    return out_at, mlp_at, w_out, mlp


def split_tail(x, o, n, w_out, gain, next_gain, w_gate, w_up, w_down, layer):
    rows, model = x.shape
    _, half, inner = o.shape
    ffn = w_gate.shape[2]
    out_steps, tf, slots = 2, TF, SLOTS
    slices = ffn // tf
    step = inner // out_steps
    steps = out_steps + slices + 1
    out_at, _, wo_spec, _ = tail_specs(layer, out_steps, slices, tf, model, step, lambda i: lax.rem(i, steps))
    hbm = pl.BlockSpec(memory_space=pl.ANY)
    part = pl.BlockSpec((half, model), lambda i: (i // steps, 0))
    full = pl.BlockSpec(gain.shape, lambda i: (0, 0))
    dma = pltpu.SemaphoreType.DMA
    return pl.pallas_call(
        functools.partial(split_kernel, n, out_steps, layer, steps),
        name="tail_split",
        grid=(2 * steps,),
        out_shape=[jax.ShapeDtypeStruct((rows, model), BF16), jax.ShapeDtypeStruct((n, half, model), BF16)],
        in_specs=[part, pl.BlockSpec((1, half, step), lambda i: (i // steps, 0, out_at(i))), wo_spec, full, full, hbm, hbm, hbm],
        out_specs=[part, pl.BlockSpec(memory_space=pl.ANY)],
        scratch_shapes=[
            pltpu.VMEM((half, model), F32),
            pltpu.VMEM((half, model), BF16),
            pltpu.VMEM((2, half, tf), BF16),
            pltpu.VMEM((half, model), BF16),
            pltpu.VMEM((slots, model, tf), BF16),
            pltpu.VMEM((slots, model, tf), BF16),
            pltpu.VMEM((slots, tf, model), BF16),
            dma((3, slots)),
            dma,
            dma((n, 2)),
            dma((6,)),
            dma((2,)),
            dma((3, 2)),
        ],
        compiler_params=pltpu.CompilerParams(vmem_limit_bytes=63 * MIB, collective_id=8 + layer, has_side_effects=True),
        cost_estimate=pl.CostEstimate(
            flops=2 * rows * model * (inner + 3 * ffn), bytes_accessed=4 * model * (inner + 3 * ffn), transcendentals=rows * ffn
        ),
    )(x, o, w_out.reshape(w_out.shape[0], inner, model), gain, next_gain, w_gate, w_up, w_down)


def last_tail(x, o, kvs, heads, w_out, gain, w_gate, w_up, w_down, layer):
    rows, model = x.shape
    _, half, inner = o.shape
    ffn = w_gate.shape[2]
    out_steps, tf = 4, TF
    slices = ffn // tf
    step = inner // out_steps
    seq, width = kvs[0].shape
    dim = width // heads
    part = seq // slices
    out_at, mlp_at, wo_spec, mlp_specs = tail_specs(layer, out_steps, slices, tf, model, step, lambda i: i)
    whole = pl.BlockSpec((rows, model), lambda i: (0, 0))
    cache = jax.ShapeDtypeStruct((layer + 1, seq * heads, dim), BF16)
    cache_spec = pl.BlockSpec((layer + 1, part * heads, dim), lambda i: (0, mlp_at(i), 0))
    return pl.pallas_call(
        functools.partial(last_kernel, out_steps, layer),
        name="tail_last",
        grid=(out_steps + slices + 1,),
        out_shape=[jax.ShapeDtypeStruct((rows, model), BF16), cache, cache],
        in_specs=[
            whole,
            pl.BlockSpec((2, half, step), lambda i: (0, 0, out_at(i))),
            wo_spec,
            pl.BlockSpec(gain.shape, lambda i: (0, 0)),
        ]
        + mlp_specs
        + [pl.BlockSpec((part, width), lambda i: (mlp_at(i), 0))] * len(kvs),
        out_specs=[whole, cache_spec, cache_spec],
        scratch_shapes=[
            pltpu.VMEM((rows, model), F32),
            pltpu.VMEM((rows, model), BF16),
            pltpu.VMEM((2, rows, tf), BF16),
            pltpu.VMEM((len(kvs), part * heads, dim), F32),
        ],
        compiler_params=pltpu.CompilerParams(vmem_limit_bytes=60 * MIB),
        cost_estimate=pl.CostEstimate(
            flops=2 * rows * model * (inner + 3 * ffn), bytes_accessed=2 * model * (inner + 3 * ffn), transcendentals=rows * ffn
        ),
    )(x, o, w_out.reshape(w_out.shape[0], inner, model), gain, w_gate, w_up, w_down, *kvs)


def solution(mesh):
    cp_size = mesh.shape["cp"]
    row_spec = P(("req", "cp"), None)
    pos_spec = P(("req", "cp"))
    rep_spec = P()
    cache_spec = P(None, "req", "cp", None)

    def per_device(hidden, positions, gain_attn, gain_mlp, w_query, w_key, w_value, w_out, w_gate, w_up, w_down):
        num_layers, model, all_heads, dim = w_query.shape
        rows = hidden.shape[0]
        cache_shape = (num_layers, cp_size * rows, all_heads // cp_size, dim)
        inv_freq = ROPE_BASE ** (-jnp.arange(0, dim, 2, dtype=F32) / dim)
        tables = [positions.reshape(rows // 128, 128), jnp.concatenate([inv_freq, inv_freq])[None]]
        kvs = []
        for layer in range(num_layers):
            o, k, v, *new = front(hidden, gain_attn, tables, w_query, w_key, w_value, cp_size, layer)
            kvs += [k, v]
            if layer == 0:
                cos_sin, new = new[:2], new[2:]
            if layer < num_layers - 1:
                hidden, gathered = split_tail(hidden, o, cp_size, w_out, gain_mlp, gain_attn, w_gate, w_up, w_down, layer)
                tables = cos_sin + new + [gathered]
            else:
                hidden, k_cache, v_cache = last_tail(
                    hidden, o, kvs, all_heads // cp_size, w_out, gain_mlp, w_gate, w_up, w_down, layer
                )
        return hidden, k_cache.reshape(cache_shape), v_cache.reshape(cache_shape)

    in_specs = (row_spec, pos_spec) + (rep_spec,) * 9
    return jax.shard_map(per_device, mesh=mesh, in_specs=in_specs, out_specs=(row_spec, cache_spec, cache_spec), check_vma=False)
```

profile of v0, /device:TPU:113, one launch (start us, length us, event | category | flops | bytes accessed | tf_op | source)
XLA Modules:
  0.0 338.9 jit_solution(1870983627340511832)
XLA Ops:
  0.6 0.6 maximum_bitcast_fusion.refs_1_
  1.2 105.7 %front.2 = (bf16[2,256,2048]{2,1,0:T(8,128)(2,1)}, bf16[4096,256]{1,0:T(8,128)(2,1)}, bf16[4096,256]{1,0:T(8,128)(2,1)}, f32[4096,128]{1,0:T(8,128)}, f32[4096,128]{1,0:T(8,128)}, /*index=5*/bf16[2048,768]{1,0:T(8,128)(2,1)}) custom-call(bf16[512,2048]{1,0:T(8,128)(2,1)} %x_ref.3, bf16[2,2048]{1,0:T(2,128)(2,1)} %gain_ref.6, s32[4,128]{1,0:T(4,128)} %bitcast.19, ...), custom_call_target="tpu_custom_call" | custom-call | flops 21474836480 | bytes 16777216 | tf_op jit(solution)/shard_map/front/pallas_call | solution.py:416
  107.0 90.8 %tail_split.1 = (bf16[512,2048]{1,0:T(8,128)(2,1)}, bf16[8,256,2048]{2,1,0:T(8,128)(2,1)}) custom-call(bf16[512,2048]{1,0:T(8,128)(2,1)} %x_ref.3, bf16[2,256,2048]{2,1,0:T(8,128)(2,1)} %get-tuple-element.17.o_ref, bf16[2,2048,2048]{2,1,0:T(8,128)(2,1)} %bitcast.9, bf16[2,2048]{1,0:T(2,128)(2,1)} %gain_ref.7, bf16[2,2048]{1,0:T(2,128)(2,1)} %gain_ref.6, ...), custom_call_target="tpu_custom_call" | custom-call | flops 55834574848 | bytes 218103808 | tf_op jit(solution)/shard_map/tail_split/pallas_call | solution.py:711
  197.8 68.1 %front.3 = (bf16[2,256,2048]{2,1,0:T(8,128)(2,1)}, bf16[4096,256]{1,0:T(8,128)(2,1)}, bf16[4096,256]{1,0:T(8,128)(2,1)}) custom-call(bf16[512,2048]{1,0:T(8,128)(2,1)} %get-tuple-element.18.x_ref, bf16[2,2048]{1,0:T(2,128)(2,1)} %gain_ref.6, f32[4096,128]{1,0:T(8,128)} %get-tuple-element.19.refs_0_, f32[4096,128]{1,0:T(8,128)} %get-tuple-element.20.refs_1_, ...), custom_call_target="tpu_custom_call" | custom-call | flops 21474836480 | bytes 16777216 | tf_op jit(solution)/shard_map/front/pallas_call | solution.py:416
  265.9 72.8 %tail_last.1 = (bf16[512,2048]{1,0:T(8,128)(2,1)}, bf16[2,8192,128]{2,1,0:T(8,128)(2,1)}, bf16[2,8192,128]{2,1,0:T(8,128)(2,1)}) custom-call(bf16[512,2048]{1,0:T(8,128)(2,1)} %get-tuple-element.18.x_ref, bf16[2,256,2048]{2,1,0:T(8,128)(2,1)} %get-tuple-element.23.o_ref, bf16[2,2048,2048]{2,1,0:T(8,128)(2,1)} %bitcast.10, bf16[2,2048]{1,0:T(2,128)(2,1)} %gain_ref.7, ...), custom_call_target="tpu_custom_call" | custom-call | flops 55834574848 | bytes 109051904 | tf_op jit(solution)/shard_map/tail_last/pallas_call | solution.py:754
  (1 shorter events, 0.0 us)
where the time goes:
time: 344 us; the launch traced here: 339 us
  Pallas kernels  337 us (98%)
    pallas_call x2, Pallas kernels, front(): pl.pallas_call(functools.partial(front_kernel, n, heads, dim, layer, firs...  174 us
    pallas_call x1, Pallas kernels, split_tail(): pl.pallas_call(functools.partial(split_kernel, n, out_steps, layer, steps...  90.8 us
    pallas_call x1, Pallas kernels, last_tail(): pl.pallas_call(functools.partial(last_kernel, out_steps, layer), name='ta...  72.8 us

commit v1 on v0

--- a/solution.py
+++ b/solution.py
@@ -194,8 +194,12 @@
         per = TK // TQ
         full = t // per
         carry = chunks(queries, 0, full, base, TK, carry)
-        carry = chunks(queries, full * per, t, base, TQ, carry)
-        carry = chunk(queries, start, TQ, carry, True)
+        carry = lax.cond(
+            t > full * per,
+            lambda c: run(queries, [(pl.multiple_of(start - TQ, TQ), TQ, False), (start, TQ, True)], c),
+            lambda c: run(queries, [(start, TQ, True)], c),
+            carry,
+        )
         for g in range(heads):
             m, l, acc = carry[g]
             o_buf[pl.ds(start, TQ), g * dim : (g + 1) * dim] = (acc / l).T.astype(BF16)

time: 344 us -> 342 us (level)
  no operation moved by 1% of the time
where the time goes in v1:
time: 342 us; the launch traced here: 337 us
  Pallas kernels  336 us (98%)
    pallas_call x2, Pallas kernels, front(): pl.pallas_call(functools.partial(front_kernel, n, heads, dim, layer, firs...  173 us
    pallas_call x1, Pallas kernels, split_tail(): pl.pallas_call(functools.partial(split_kernel, n, out_steps, layer, steps...  90 us
    pallas_call x1, Pallas kernels, last_tail(): pl.pallas_call(functools.partial(last_kernel, out_steps, layer), name='ta...  72.8 us

profile of v1, /device:TPU:113, one launch (start us, length us, event | category | flops | bytes accessed | tf_op | source)
XLA Modules:
  0.0 337.1 jit_solution(11481139209865307196)
XLA Ops:
  0.6 0.6 maximum_bitcast_fusion.refs_1_
  1.2 105.3 %front.2 = (bf16[2,256,2048]{2,1,0:T(8,128)(2,1)}, bf16[4096,256]{1,0:T(8,128)(2,1)}, bf16[4096,256]{1,0:T(8,128)(2,1)}, f32[4096,128]{1,0:T(8,128)}, f32[4096,128]{1,0:T(8,128)}, /*index=5*/bf16[2048,768]{1,0:T(8,128)(2,1)}) custom-call(bf16[512,2048]{1,0:T(8,128)(2,1)} %x_ref.3, bf16[2,2048]{1,0:T(2,128)(2,1)} %gain_ref.6, s32[4,128]{1,0:T(4,128)} %bitcast.19, ...), custom_call_target="tpu_custom_call" | custom-call | flops 21474836480 | bytes 16777216 | tf_op jit(solution)/shard_map/front/pallas_call | solution.py:420
  106.6 90.0 %tail_split.1 = (bf16[512,2048]{1,0:T(8,128)(2,1)}, bf16[8,256,2048]{2,1,0:T(8,128)(2,1)}) custom-call(bf16[512,2048]{1,0:T(8,128)(2,1)} %x_ref.3, bf16[2,256,2048]{2,1,0:T(8,128)(2,1)} %get-tuple-element.17.o_ref, bf16[2,2048,2048]{2,1,0:T(8,128)(2,1)} %bitcast.9, bf16[2,2048]{1,0:T(2,128)(2,1)} %gain_ref.7, bf16[2,2048]{1,0:T(2,128)(2,1)} %gain_ref.6, ...), custom_call_target="tpu_custom_call" | custom-call | flops 55834574848 | bytes 218103808 | tf_op jit(solution)/shard_map/tail_split/pallas_call | solution.py:715
  196.6 67.5 %front.3 = (bf16[2,256,2048]{2,1,0:T(8,128)(2,1)}, bf16[4096,256]{1,0:T(8,128)(2,1)}, bf16[4096,256]{1,0:T(8,128)(2,1)}) custom-call(bf16[512,2048]{1,0:T(8,128)(2,1)} %get-tuple-element.18.x_ref, bf16[2,2048]{1,0:T(2,128)(2,1)} %gain_ref.6, f32[4096,128]{1,0:T(8,128)} %get-tuple-element.19.refs_0_, f32[4096,128]{1,0:T(8,128)} %get-tuple-element.20.refs_1_, ...), custom_call_target="tpu_custom_call" | custom-call | flops 21474836480 | bytes 16777216 | tf_op jit(solution)/shard_map/front/pallas_call | solution.py:420
  264.1 72.8 %tail_last.1 = (bf16[512,2048]{1,0:T(8,128)(2,1)}, bf16[2,8192,128]{2,1,0:T(8,128)(2,1)}, bf16[2,8192,128]{2,1,0:T(8,128)(2,1)}) custom-call(bf16[512,2048]{1,0:T(8,128)(2,1)} %get-tuple-element.18.x_ref, bf16[2,256,2048]{2,1,0:T(8,128)(2,1)} %get-tuple-element.23.o_ref, bf16[2,2048,2048]{2,1,0:T(8,128)(2,1)} %bitcast.10, bf16[2,2048]{1,0:T(2,128)(2,1)} %gain_ref.7, ...), custom_call_target="tpu_custom_call" | custom-call | flops 55834574848 | bytes 109051904 | tf_op jit(solution)/shard_map/tail_last/pallas_call | solution.py:758
  (1 shorter events, 0.0 us)
